TPU v7x, 128 devices: a whole 4x4x4 slice. The times are simulated.
128 devices in a mesh: gx: 8 (over y, core), gy: 4 (over z), gz: 4 (over x).
Axes of the slice: x: 4, y: 4, z: 4, core: 2. Of those that a mesh axis runs over, the one named last changes fastest.
Arguments:
- kappa_sq: float32 [128, 64, 512], P('gx', 'gz', 'gy'), may hold values from 0.004 to 0.4
- probe_bits: int32 [4, 128, 64, 512], P(None, 'gx', 'gz', 'gy'), may hold values from 0 to 1
Outputs:
- solution: float32 [4, 128, 64, 512], P(None, 'gx', 'gz', 'gy')
- relative_residual: float32 [4], replicated
All inputs are finite; a program needn't handle non-finite values.
Results may differ from a plain program's by a relative error of at most 0.0001.
Values sent between devices are 32-bit elements; how exact they have to be, the bound alone decides.
A program may use at most 128 MiB of HBM per device.

v0:
```python
import jax
import jax.numpy as jnp
from jax import lax
from jax.sharding import Mesh
from jax.sharding import PartitionSpec as P

LEVELS = 3
COARSE_SWEEPS = 8
ITERS = 2
GX_GY_GZ = ("gx_0", "gx_1", "gy", "gz")
GX = ("gx_0", "gx_1")
damping = 0.8


def extended(block, sides, width):
    for axis, dim in sides:
        count = lax.axis_size(axis)
        forward = [(i, i + 1) for i in range(count - 1)]
        backward = [(target, source) for source, target in forward]
        low = lax.ppermute(
            lax.slice_in_dim(block, block.shape[dim] - width, None, axis=dim), axis, forward
        )
        high = lax.ppermute(lax.slice_in_dim(block, 0, width, axis=dim), axis, backward)
        block = jnp.concatenate([low, block, high], axis=dim)
    return block


def extended_2(value, sides, width):
    edges = {}
    for axis, dim in sides:
        size, length = (lax.axis_size(axis), value.shape[dim])
        up = [(i, (i + 1) % size) for i in range(size - 1)]
        last = lax.slice_in_dim(value, length - width, length, axis=dim)
        first = lax.slice_in_dim(value, 0, width, axis=dim)
        edges[dim] = (
            lax.ppermute(last, axis, up),
            lax.ppermute(first, axis, [(b, a) for a, b in up]),
        )
    done = []
    for _, dim in sides:
        low, high = edges[dim]
        around = [(width, width) if d in done else (0, 0) for d in range(value.ndim)]
        value = jnp.concatenate([jnp.pad(low, around), value, jnp.pad(high, around)], axis=dim)
        done.append(dim)
    return value


def over_axes(value, axes):
    for axis in axes:
        value = lax.psum(value, axis)
    return value


def neighbours(padded):
    along_first = padded[..., 2:, 1:-1, 1:-1] + padded[..., :-2, 1:-1, 1:-1]
    along_second = padded[..., 1:-1, 2:, 1:-1] + padded[..., 1:-1, :-2, 1:-1]
    along_third = padded[..., 1:-1, 1:-1, 2:] + padded[..., 1:-1, 1:-1, :-2]
    return along_first + along_second + along_third


def coarsen(field):
    leading = field.shape[:-3]
    cells_first, cells_second, cells_third = field.shape[-3:]
    grouped = field.reshape(
        leading + (cells_first // 2, 2, cells_second // 2, 2, cells_third // 2, 2)
    )
    return jnp.mean(grouped, axis=(-5, -3, -1))


def refine(field):
    leading = field.shape[:-3]
    cells_first, cells_second, cells_third = field.shape[-3:]
    spread = field.reshape(leading + (cells_first, 1, cells_second, 1, cells_third, 1))
    spread = jnp.broadcast_to(spread, leading + (cells_first, 2, cells_second, 2, cells_third, 2))
    return spread.reshape(leading + (cells_first * 2, cells_second * 2, cells_third * 2))


def level_faces(field, grid_level):
    if grid_level == 0:
        return extended(field, ((GX, 1), ("gy", 3), ("gz", 2)), 1)
    return extended_2(field, ((GX, 1), ("gy", 3), ("gz", 2)), 1)


def operate(field, diagonal, coupling, grid_level):
    return diagonal * field - coupling * neighbours(level_faces(field, grid_level))


def jacobi_sweep(field, rhs_field, diagonal, coupling, grid_level):
    return field + damping * (rhs_field - operate(field, diagonal, coupling, grid_level)) / diagonal


def assemble(gathered):
    count_x = lax.axis_size(GX)
    count_y = lax.axis_size("gy")
    count_z = lax.axis_size("gz")
    leading = gathered.shape[1:-3]
    cells_first, cells_second, cells_third = gathered.shape[-3:]
    lead_count = len(leading)
    blocks = gathered.reshape(
        (count_x, count_y, count_z) + leading + (cells_first, cells_second, cells_third)
    )
    permutation = tuple(range(3, 3 + lead_count)) + (
        0,
        3 + lead_count,
        2,
        4 + lead_count,
        1,
        5 + lead_count,
    )
    blocks = jnp.transpose(blocks, permutation)
    return blocks.reshape(
        leading + (count_x * cells_first, count_z * cells_second, count_y * cells_third)
    )


def local_dot(first_field, second_field):
    return jnp.sum(first_field * second_field, axis=(1, 2, 3))


def expand(values):
    return values[:, None, None, None]


def per_device(kappa_sq, probe_bits):
    diagonals = []
    couplings = []
    coef_field = kappa_sq
    for grid_level in range(LEVELS + 1):
        if grid_level > 0:
            coef_field = coarsen(coef_field)
        coupling = 0.25**grid_level
        diagonals.append(coef_field + 6.0 * coupling)
        couplings.append(coupling)
    global_diag = assemble(lax.all_gather(diagonals[LEVELS][None], GX_GY_GZ, axis=0, tiled=True))

    def coarsest(rhs_field):
        diagonal = diagonals[LEVELS]
        coupling = couplings[LEVELS]
        global_rhs = assemble(lax.all_gather(rhs_field[None], GX_GY_GZ, axis=0, tiled=True))
        field = damping * global_rhs / global_diag
        for sweep_index in range(COARSE_SWEEPS - 1):
            padded = jnp.pad(field, ((0, 0), (1, 1), (1, 1), (1, 1)))
            field = (
                field
                + damping
                * (global_rhs - (global_diag * field - coupling * neighbours(padded)))
                / global_diag
            )
        probes, block_x, block_z, block_y = rhs_field.shape
        zero_index = jnp.zeros((), jnp.int32)
        starts = (
            zero_index,
            lax.axis_index(GX) * block_x,
            lax.axis_index("gz") * block_z,
            lax.axis_index("gy") * block_y,
        )
        return lax.dynamic_slice(field, starts, (probes, block_x, block_z, block_y))

    def vcycle(rhs_field, grid_level):
        if grid_level == LEVELS:
            return coarsest(rhs_field)
        diagonal = diagonals[grid_level]
        coupling = couplings[grid_level]
        field = damping * rhs_field / diagonal
        field = jacobi_sweep(field, rhs_field, diagonal, coupling, grid_level)
        remainder = rhs_field - operate(field, diagonal, coupling, grid_level)
        field = field + refine(vcycle(coarsen(remainder), grid_level + 1))
        field = jacobi_sweep(field, rhs_field, diagonal, coupling, grid_level)
        return jacobi_sweep(field, rhs_field, diagonal, coupling, grid_level)

    right_side = 2.0 * probe_bits.astype(jnp.float32) - 1.0
    solution = jnp.zeros_like(right_side)
    residual = right_side
    fine_diag = diagonals[0]

    def pair_sums(residual_now, precond_now, operated_now):
        return (
            over_axes(local_dot(residual_now, precond_now), GX_GY_GZ),
            over_axes(local_dot(precond_now, operated_now), GX_GY_GZ),
        )

    precond = vcycle(residual, 0)
    operated = operate(precond, fine_diag, 1.0, 0)
    precond_dot, curve_dot = pair_sums(residual, precond, operated)
    step_size = precond_dot / curve_dot
    search = precond
    along = operated
    for iteration in range(ITERS):
        solution = solution + expand(step_size) * search
        residual = residual - expand(step_size) * along
        if iteration + 1 < ITERS:
            precond = vcycle(residual, 0)
            operated = operate(precond, fine_diag, 1.0, 0)
            next_dot, curve_dot = pair_sums(residual, precond, operated)
            ratio_next = next_dot / precond_dot
            step_size = next_dot / (curve_dot - ratio_next * next_dot / step_size)
            search = precond + expand(ratio_next) * search
            along = operated + expand(ratio_next) * along
            precond_dot = next_dot
    squares = lax.psum(local_dot(residual, residual), GX_GY_GZ)
    cell_total = (
        probe_bits.shape[1]
        * probe_bits.shape[2]
        * probe_bits.shape[3]
        * lax.axis_size(GX)
        * lax.axis_size("gy")
        * lax.axis_size("gz")
    )
    return (solution, jnp.sqrt(squares / cell_total))


def solution(mesh):
    finer = Mesh(
        mesh.devices.reshape(4, 2, mesh.shape["gy"], mesh.shape["gz"]), ("gx_0", "gx_1", "gy", "gz")
    )
    placed = (P(GX, "gz", "gy"), P(None, GX, "gz", "gy"))
    return jax.shard_map(
        per_device,
        mesh=finer,
        in_specs=placed,
        out_specs=(P(None, GX, "gz", "gy"), P()),
        check_vma=False,
    )
```

profile of v0, /device:TPU:1, one launch (start us, length us, event | category | flops | bytes accessed | tf_op | source)
XLA Modules:
  0.0 1092.7 jit_solution(3623767073840948052)
XLA Ops:
  37.2 9.7 reshape.124
  72.7 8.8 copy.2403
  81.5 13.1 %reduce_sum.126 = f32[4,8,8,64]{0,3,2,1:T(8,128)} reduce(f32[4,8,2,8,2,64,2]{0,6,5,4,3,2,1:T(2,128)} %bitcast.21, f32[]{:T(128)} %constant.28.clone.1), dimensions={2,4,6}, to_apply=%region_0.0 | reduce | flops 114688 | bytes 589828 | tf_op jit(solution)/shard_map/reduce_sum | solution.py:67
  131.7 62.1 %all-gather.1 = f32[256,2,16]{2,1,0:T(2,128)S(1)} all-gather(f32[2,2,16]{2,1,0:T(2,128)S(1)} %multiply_add_fusion.2), channel_id=3, replica_groups=mesh['gx_0'=4,'gx_1'=2,'gy'=4,'gz'=4] {'gx_0','gx_1','gy','gz'}, dimensions={0}, use_global_device_ids=true | all-gather | bytes 33024 | tf_op jit(solution)/shard_map/all_gather | solution.py:134
  244.9 61.7 %all-gather = f32[512,2,2,16]{3,2,1,0:T(2,128)S(1)} all-gather(f32[4,2,2,16]{3,2,1,0:T(2,128)S(1)} %copy.2408), channel_id=2, replica_groups=mesh['gx_0'=4,'gx_1'=2,'gy'=4,'gz'=4] {'gx_0','gx_1','gy','gz'}, dimensions={0}, use_global_device_ids=true | all-gather | bytes 132096 | tf_op jit(solution)/shard_map/all_gather | solution.py:139
  354.4 6.2 collective-permute-start.49
  380.1 6.2 collective-permute-start.55
  407.8 9.0 broadcast_in_dim.14
  416.8 10.0 copy.2416
  426.9 6.2 collective-permute-start.61
  510.5 7.5 all-reduce.83
  524.0 10.6 all-reduce.81
  601.5 8.8 copy.2467
  610.3 13.1 %reduce_sum.134 = f32[4,8,8,64]{0,3,2,1:T(8,128)} reduce(f32[4,8,2,8,2,64,2]{0,6,5,4,3,2,1:T(2,128)} %bitcast.23, f32[]{:T(128)} %constant.28.clone.1), dimensions={2,4,6}, to_apply=%region_16.17 | reduce | flops 114688 | bytes 589828 | tf_op jit(solution)/shard_map/reduce_sum | solution.py:67
  703.5 6.2 collective-permute-start.109
  726.6 60.6 %all-gather.2 = f32[512,2,2,16]{3,2,1,0:T(2,128)S(1)} all-gather(f32[4,2,2,16]{3,2,1,0:T(2,128)S(1)} %copy.2472), channel_id=4, replica_groups=mesh['gx_0'=4,'gx_1'=2,'gy'=4,'gz'=4] {'gx_0','gx_1','gy','gz'}, dimensions={0}, use_global_device_ids=true | all-gather | bytes 132096 | tf_op jit(solution)/shard_map/all_gather | solution.py:139
  837.4 6.2 collective-permute-start.127
  862.9 6.2 collective-permute-start.133
  890.6 9.0 broadcast_in_dim.17
  899.6 10.0 copy.2478
  909.7 6.2 collective-permute-start.139
  994.2 7.5 all-reduce.82
  1007.7 10.6 all-reduce.80
  1026.5 65.5 %psum.135 = f32[4]{0:T(128)S(1)} all-reduce(f32[4]{0:T(128)S(1)} %get-tuple-element.200), channel_id=1, replica_groups=mesh['gx_0'=4,'gx_1'=2,'gy'=4,'gz'=4] {'gx_0','gx_1','gy','gz'}, use_global_device_ids=true, to_apply=%region_30.31 | all-reduce | flops 4 | bytes 32 | tf_op jit(solution)/shard_map/psum | solution.py:200
  (630 shorter events, 667.4 us)
Async XLA Ops:
  31.1 20.0 %collective-permute-start.7 = (f32[4,1,16,128]{3,2,1,0:T(8,128)S(1)}, f32[4,1,16,128]{3,2,1,0:T(8,128)S(1)}, u32[]{:S(2)}, u32[]{:S(2)}) collective-permute-start(f32[4,1,16,128]{3,2,1,0:T(8,128)S(1)} %get-tuple-element.96), channel_id=1, source_target_pairs={{0,16},{16,32},{32,48},{48,64},{64,80},{80,96},{96,112},{1,17},{17... | collective-permute-start | bytes 98312 | tf_op jit(solution)/shard_map/ppermute | solution.py:20
  98.4 19.2 %collective-permute-start.13 = (f32[4,1,8,64]{3,2,1,0:T(8,128)S(1)}, f32[4,1,8,64]{3,2,1,0:T(8,128)S(1)}, u32[]{:S(2)}, u32[]{:S(2)}) collective-permute-start(f32[4,1,8,64]{3,2,1,0:T(8,128)S(1)} %get-tuple-element.194), channel_id=1, source_target_pairs={{0,16},{16,32},{32,48},{48,64},{64,80},{80,96},{96,112},{1,17},{17... | collective-permute-start | bytes 24584 | tf_op jit(solution)/shard_map/ppermute | solution.py:36
  118.1 79.0 %collective-permute-start.19 = (f32[4,1,8,64]{3,2,1,0:T(8,128)S(1)}, f32[4,1,8,64]{3,2,1,0:T(8,128)S(1)}, u32[]{:S(2)}, u32[]{:S(2)}) collective-permute-start(f32[4,1,8,64]{3,2,1,0:T(8,128)S(1)} %get-tuple-element.188), channel_id=1, source_target_pairs={{0,16},{16,32},{32,48},{48,64},{64,80},{80,96},{96,112},{1,17},{17... | collective-permute-start | bytes 24584 | tf_op jit(solution)/shard_map/ppermute | solution.py:36
  123.1 73.9 %collective-permute-start.18 = (f32[4,1,8,64]{3,2,1,0:T(8,128)S(1)}, f32[4,1,8,64]{3,2,1,0:T(8,128)S(1)}, u32[]{:S(2)}, u32[]{:S(2)}) collective-permute-start(f32[4,1,8,64]{3,2,1,0:T(8,128)S(1)} %get-tuple-element.189), channel_id=1, source_target_pairs={{16,0},{32,16},{48,32},{64,48},{80,64},{96,80},{112,96},{17,1},{33... | collective-permute-start | bytes 24584 | tf_op jit(solution)/shard_map/ppermute | solution.py:37
  125.1 72.0 %collective-permute-start.22 = (f32[4,8,1,64]{3,2,1,0:T(1,128)S(1)}, f32[4,8,1,64]{3,2,1,0:T(1,128)S(1)}, u32[]{:S(2)}, u32[]{:S(2)}) collective-permute-start(f32[4,8,1,64]{3,2,1,0:T(1,128)S(1)} %get-tuple-element.184), channel_id=1, source_target_pairs={{1,0},{2,1},{3,2},{5,4},{6,5},{7,6},{9,8},{10,9},{11,10},{13,12},{... | collective-permute-start | bytes 24584 | tf_op jit(solution)/shard_map/ppermute | solution.py:37
  126.4 70.7 %collective-permute-start.23 = (f32[4,8,1,64]{3,2,1,0:T(1,128)S(1)}, f32[4,8,1,64]{3,2,1,0:T(1,128)S(1)}, u32[]{:S(2)}, u32[]{:S(2)}) collective-permute-start(f32[4,8,1,64]{3,2,1,0:T(1,128)S(1)} %get-tuple-element.185), channel_id=1, source_target_pairs={{0,1},{1,2},{2,3},{4,5},{5,6},{6,7},{8,9},{9,10},{10,11},{12,13},{... | collective-permute-start | bytes 24584 | tf_op jit(solution)/shard_map/ppermute | solution.py:36
  130.4 63.4 %collective-permute-start.21 = (f32[4,8,8,1]{3,2,1,0:T(8,128)S(1)}, f32[4,8,8,1]{3,2,1,0:T(8,128)S(1)}, u32[]{:S(2)}, u32[]{:S(2)}) collective-permute-start(f32[4,8,8,1]{3,2,1,0:T(8,128)S(1)} %get-tuple-element.186), channel_id=1, source_target_pairs={{4,0},{8,4},{12,8},{5,1},{9,5},{13,9},{6,2},{10,6},{14,10},{7,3},{... | collective-permute-start | bytes 3080 | tf_op jit(solution)/shard_map/ppermute | solution.py:37
  202.6 20.1 %collective-permute-start.25 = (f32[4,1,4,32]{0,3,2,1:T(8,128)S(1)}, f32[4,1,4,32]{0,3,2,1:T(8,128)S(1)}, u32[]{:S(2)}, u32[]{:S(2)}) collective-permute-start(f32[4,1,4,32]{0,3,2,1:T(8,128)S(1)} %get-tuple-element.146), channel_id=1, source_target_pairs={{0,16},{16,32},{32,48},{48,64},{64,80},{80,96},{96,112},{1,17},{17... | collective-permute-start | bytes 6152 | tf_op jit(solution)/shard_map/ppermute | solution.py:36
  223.0 21.3 %collective-permute-start.31 = (f32[4,1,4,32]{0,3,2,1:T(8,128)S(1)}, f32[4,1,4,32]{0,3,2,1:T(8,128)S(1)}, u32[]{:S(2)}, u32[]{:S(2)}) collective-permute-start(f32[4,1,4,32]{0,3,2,1:T(8,128)S(1)} %get-tuple-element.140), channel_id=1, source_target_pairs={{0,16},{16,32},{32,48},{48,64},{64,80},{80,96},{96,112},{1,17},{17... | collective-permute-start | bytes 6152 | tf_op jit(solution)/shard_map/ppermute | solution.py:36
  327.3 22.1 %collective-permute-start.43 = (f32[4,1,4,32]{0,3,2,1:T(8,128)S(1)}, f32[4,1,4,32]{0,3,2,1:T(8,128)S(1)}, u32[]{:S(2)}, u32[]{:S(2)}) collective-permute-start(f32[4,1,4,32]{0,3,2,1:T(8,128)S(1)} %get-tuple-element.128), channel_id=1, source_target_pairs={{0,16},{16,32},{32,48},{48,64},{64,80},{80,96},{96,112},{1,17},{17... | collective-permute-start | bytes 6152 | tf_op jit(solution)/shard_map/ppermute | solution.py:36
  354.4 25.3 %collective-permute-start.49 = (f32[4,1,8,64]{3,2,1,0:T(8,128)S(1)}, f32[4,1,8,64]{3,2,1,0:T(8,128)S(1)}, u32[]{:S(2)}, u32[]{:S(2)}) collective-permute-start(f32[4,1,8,64]{3,2,1,0:T(8,128)S(1)} %get-tuple-element.182), channel_id=1, source_target_pairs={{0,16},{16,32},{32,48},{48,64},{64,80},{80,96},{96,112},{1,17},{17... | collective-permute-start | bytes 24584 | tf_op jit(solution)/shard_map/ppermute | solution.py:36
  360.6 19.1 %collective-permute-start.48 = (f32[4,1,8,64]{3,2,1,0:T(8,128)S(1)}, f32[4,1,8,64]{3,2,1,0:T(8,128)S(1)}, u32[]{:S(2)}, u32[]{:S(2)}) collective-permute-start(f32[4,1,8,64]{3,2,1,0:T(8,128)S(1)} %get-tuple-element.183), channel_id=1, source_target_pairs={{16,0},{32,16},{48,32},{64,48},{80,64},{96,80},{112,96},{17,1},{33... | collective-permute-start | bytes 24584 | tf_op jit(solution)/shard_map/ppermute | solution.py:37
  380.1 25.3 %collective-permute-start.55 = (f32[4,1,8,64]{3,2,1,0:T(8,128)S(1)}, f32[4,1,8,64]{3,2,1,0:T(8,128)S(1)}, u32[]{:S(2)}, u32[]{:S(2)}) collective-permute-start(f32[4,1,8,64]{3,2,1,0:T(8,128)S(1)} %get-tuple-element.176), channel_id=1, source_target_pairs={{0,16},{16,32},{32,48},{48,64},{64,80},{80,96},{96,112},{1,17},{17... | collective-permute-start | bytes 24584 | tf_op jit(solution)/shard_map/ppermute | solution.py:36
  386.3 19.1 %collective-permute-start.54 = (f32[4,1,8,64]{3,2,1,0:T(8,128)S(1)}, f32[4,1,8,64]{3,2,1,0:T(8,128)S(1)}, u32[]{:S(2)}, u32[]{:S(2)}) collective-permute-start(f32[4,1,8,64]{3,2,1,0:T(8,128)S(1)} %get-tuple-element.177), channel_id=1, source_target_pairs={{16,0},{32,16},{48,32},{64,48},{80,64},{96,80},{112,96},{17,1},{33... | collective-permute-start | bytes 24584 | tf_op jit(solution)/shard_map/ppermute | solution.py:37
  625.7 25.1 %collective-permute-start.91 = (f32[4,1,8,64]{3,2,1,0:T(8,128)S(1)}, f32[4,1,8,64]{3,2,1,0:T(8,128)S(1)}, u32[]{:S(2)}, u32[]{:S(2)}) collective-permute-start(f32[4,1,8,64]{3,2,1,0:T(8,128)S(1)} %get-tuple-element.170), channel_id=1, source_target_pairs={{0,16},{16,32},{32,48},{48,64},{64,80},{80,96},{96,112},{1,17},{17... | collective-permute-start | bytes 24584 | tf_op jit(solution)/shard_map/ppermute | solution.py:36
  629.8 21.1 %collective-permute-start.90 = (f32[4,1,8,64]{3,2,1,0:T(8,128)S(1)}, f32[4,1,8,64]{3,2,1,0:T(8,128)S(1)}, u32[]{:S(2)}, u32[]{:S(2)}) collective-permute-start(f32[4,1,8,64]{3,2,1,0:T(8,128)S(1)} %get-tuple-element.171), channel_id=1, source_target_pairs={{16,0},{32,16},{48,32},{64,48},{80,64},{96,80},{112,96},{17,1},{33... | collective-permute-start | bytes 24584 | tf_op jit(solution)/shard_map/ppermute | solution.py:37
  631.7 19.1 %collective-permute-start.94 = (f32[4,8,1,64]{3,2,1,0:T(1,128)S(1)}, f32[4,8,1,64]{3,2,1,0:T(1,128)S(1)}, u32[]{:S(2)}, u32[]{:S(2)}) collective-permute-start(f32[4,8,1,64]{3,2,1,0:T(1,128)S(1)} %get-tuple-element.166), channel_id=1, source_target_pairs={{1,0},{2,1},{3,2},{5,4},{6,5},{7,6},{9,8},{10,9},{11,10},{13,12},{... | collective-permute-start | bytes 24584 | tf_op jit(solution)/shard_map/ppermute | solution.py:37
  651.2 24.3 %collective-permute-start.97 = (f32[4,1,8,64]{3,2,1,0:T(8,128)S(1)}, f32[4,1,8,64]{3,2,1,0:T(8,128)S(1)}, u32[]{:S(2)}, u32[]{:S(2)}) collective-permute-start(f32[4,1,8,64]{3,2,1,0:T(8,128)S(1)} %get-tuple-element.164), channel_id=1, source_target_pairs={{0,16},{16,32},{32,48},{48,64},{64,80},{80,96},{96,112},{1,17},{17... | collective-permute-start | bytes 24584 | tf_op jit(solution)/shard_map/ppermute | solution.py:36
  655.9 19.6 %collective-permute-start.96 = (f32[4,1,8,64]{3,2,1,0:T(8,128)S(1)}, f32[4,1,8,64]{3,2,1,0:T(8,128)S(1)}, u32[]{:S(2)}, u32[]{:S(2)}) collective-permute-start(f32[4,1,8,64]{3,2,1,0:T(8,128)S(1)} %get-tuple-element.165), channel_id=1, source_target_pairs={{16,0},{32,16},{48,32},{64,48},{80,64},{96,80},{112,96},{17,1},{33... | collective-permute-start | bytes 24584 | tf_op jit(solution)/shard_map/ppermute | solution.py:37
  681.1 22.1 %collective-permute-start.103 = (f32[4,1,4,32]{0,3,2,1:T(8,128)S(1)}, f32[4,1,4,32]{0,3,2,1:T(8,128)S(1)}, u32[]{:S(2)}, u32[]{:S(2)}) collective-permute-start(f32[4,1,4,32]{0,3,2,1:T(8,128)S(1)} %get-tuple-element.122), channel_id=1, source_target_pairs={{0,16},{16,32},{32,48},{48,64},{64,80},{80,96},{96,112},{1,17},{17... | collective-permute-start | bytes 6152 | tf_op jit(solution)/shard_map/ppermute | solution.py:36
  703.5 22.6 %collective-permute-start.109 = (f32[4,1,4,32]{0,3,2,1:T(8,128)S(1)}, f32[4,1,4,32]{0,3,2,1:T(8,128)S(1)}, u32[]{:S(2)}, u32[]{:S(2)}) collective-permute-start(f32[4,1,4,32]{0,3,2,1:T(8,128)S(1)} %get-tuple-element.116), channel_id=1, source_target_pairs={{0,16},{16,32},{32,48},{48,64},{64,80},{80,96},{96,112},{1,17},{17... | collective-permute-start | bytes 6152 | tf_op jit(solution)/shard_map/ppermute | solution.py:36
  810.3 22.1 %collective-permute-start.121 = (f32[4,1,4,32]{0,3,2,1:T(8,128)S(1)}, f32[4,1,4,32]{0,3,2,1:T(8,128)S(1)}, u32[]{:S(2)}, u32[]{:S(2)}) collective-permute-start(f32[4,1,4,32]{0,3,2,1:T(8,128)S(1)} %get-tuple-element.104), channel_id=1, source_target_pairs={{0,16},{16,32},{32,48},{48,64},{64,80},{80,96},{96,112},{1,17},{17... | collective-permute-start | bytes 6152 | tf_op jit(solution)/shard_map/ppermute | solution.py:36
  837.4 25.1 %collective-permute-start.127 = (f32[4,1,8,64]{3,2,1,0:T(8,128)S(1)}, f32[4,1,8,64]{3,2,1,0:T(8,128)S(1)}, u32[]{:S(2)}, u32[]{:S(2)}) collective-permute-start(f32[4,1,8,64]{3,2,1,0:T(8,128)S(1)} %get-tuple-element.158), channel_id=1, source_target_pairs={{0,16},{16,32},{32,48},{48,64},{64,80},{80,96},{96,112},{1,17},{17... | collective-permute-start | bytes 24584 | tf_op jit(solution)/shard_map/ppermute | solution.py:36
  862.9 25.3 %collective-permute-start.133 = (f32[4,1,8,64]{3,2,1,0:T(8,128)S(1)}, f32[4,1,8,64]{3,2,1,0:T(8,128)S(1)}, u32[]{:S(2)}, u32[]{:S(2)}) collective-permute-start(f32[4,1,8,64]{3,2,1,0:T(8,128)S(1)} %get-tuple-element.152), channel_id=1, source_target_pairs={{0,16},{16,32},{32,48},{48,64},{64,80},{80,96},{96,112},{1,17},{17... | collective-permute-start | bytes 24584 | tf_op jit(solution)/shard_map/ppermute | solution.py:36
  (142 other events, 1379.7 us)
where the time goes:
time: 1110 us; the launch traced here: 1090 us
  starting transfers between devices  431 us (39%)
  blocking collectives  310 us (28%)
  waiting for transfers between devices  159 us (14%)
  local copies, waits for them, and re-layouts  122 us (11%)
  other arithmetic  67.4 us (6%)
    ppermute x48, starting transfers between devices, extended_2(): lax.ppermute(last, axis, up)  195 us
    all_gather x2, blocking collectives, coarsest(): lax.all_gather(rhs_field[None], GX_GY_GZ, axis=0, tiled=True)  122 us
    ppermute x30, starting transfers between devices, extended(): lax.ppermute(lax.slice_in_dim(block, block.shape[dim] - width, None, axis...  116 us
    ppermute x48, starting transfers between devices, extended_2(): lax.ppermute(first, axis, [(b, a) for a, b in up])  74.5 us
    ppermute x30, waiting for transfers between devices, extended(): lax.ppermute(lax.slice_in_dim(block, 0, width, axis=dim), axis, backward)  71.7 us
    psum x1, blocking collectives, per_device(): squares = lax.psum(local_dot(residual, residual), GX_GY_GZ)  65.5 us
    all_gather x1, blocking collectives, per_device(): lax.all_gather(diagonals[LEVELS][None], GX_GY_GZ, axis=0, tiled=True)  62.1 us
    psum x8, blocking collectives, over_axes(): value = lax.psum(value, axis)  60.2 us
  transfers between devices with their start and end apart: 156, of which 68 were waited for; matrix products, arithmetic and copies ran while one was open for 2% of the time, Pallas kernels for 0%

commit v1 on v0

--- a/solution.py
+++ b/solution.py
@@ -136,7 +136,14 @@
     def coarsest(rhs_field):
         diagonal = diagonals[LEVELS]
         coupling = couplings[LEVELS]
-        global_rhs = assemble(lax.all_gather(rhs_field[None], GX_GY_GZ, axis=0, tiled=True))
+
+        def close_the_sector(view):
+            mixed_arr = lax.axis_size(GX_GY_GZ)
+            all_values = jnp.stack([view] * mixed_arr, 0)
+            built = lax.all_to_all(all_values, GX_GY_GZ, 0, 0)
+            return jnp.concatenate(built, 0)
+
+        global_rhs = assemble(close_the_sector(rhs_field[None]))
         field = damping * global_rhs / global_diag
         for sweep_index in range(COARSE_SWEEPS - 1):
             padded = jnp.pad(field, ((0, 0), (1, 1), (1, 1), (1, 1)))

time: 1110 us -> 1040 us (0.937)
  blocking collectives: 310 us -> 208 us
  starting transfers between devices: 431 us -> 445 us
  local copies, waits for them, and re-layouts: 122 us -> 134 us
    all_gather x2 -> x0, blocking collectives: 122 us -> none  [coarsest(): lax.all_gather(rhs_field[None], GX_GY_GZ, axis=0, tiled=True)]
    all_to_all x0 -> x1, blocking collectives: none -> 21 us  [close_the_sector(): built = lax.all_to_all(all_values, GX_GY_GZ, 0, 0)]
    all_to_all x0 -> x1, starting transfers between devices: none -> 11.4 us  [close_the_sector(): built = lax.all_to_all(all_values, GX_GY_GZ, 0, 0)]
  transfers between devices with their start and end apart: 156 -> 157, of which waited for: 68 -> 69; matrix products, arithmetic and copies ran while one was open for 2% -> 3% of each run, Pallas kernels for 0% -> 0%
where the time goes in v1:
time: 1040 us; the launch traced here: 1020 us
  starting transfers between devices  445 us (43%)
  blocking collectives  208 us (20%)
  waiting for transfers between devices  162 us (16%)
  local copies, waits for them, and re-layouts  134 us (13%)
  other arithmetic  69.2 us (7%)
    ppermute x48, starting transfers between devices, extended_2(): lax.ppermute(last, axis, up)  200 us
    ppermute x30, starting transfers between devices, extended(): lax.ppermute(lax.slice_in_dim(block, block.shape[dim] - width, None, axis...  116 us
    ppermute x48, starting transfers between devices, extended_2(): lax.ppermute(first, axis, [(b, a) for a, b in up])  72.7 us
    ppermute x30, waiting for transfers between devices, extended(): lax.ppermute(lax.slice_in_dim(block, 0, width, axis=dim), axis, backward)  72 us
    psum x1, blocking collectives, per_device(): squares = lax.psum(local_dot(residual, residual), GX_GY_GZ)  65.5 us
    ppermute x48, waiting for transfers between devices, extended_2(): lax.ppermute(first, axis, [(b, a) for a, b in up])  63.7 us
    all_gather x1, blocking collectives, per_device(): lax.all_gather(diagonals[LEVELS][None], GX_GY_GZ, axis=0, tiled=True)  62 us
    psum x8, blocking collectives, over_axes(): value = lax.psum(value, axis)  59.2 us
  transfers between devices with their start and end apart: 157, of which 69 were waited for; matrix products, arithmetic and copies ran while one was open for 3% of the time, Pallas kernels for 0%

profile of v1, /device:TPU:1, one launch (start us, length us, event | category | flops | bytes accessed | tf_op | source)
XLA Modules:
  0.0 1022.6 jit_solution(9989817607021942956)
XLA Ops:
  47.2 9.7 reshape.112
  71.9 8.7 copy.2403
  80.6 13.1 %reduce_sum.126 = f32[4,8,8,64]{0,3,2,1:T(8,128)} reduce(f32[4,8,2,8,2,64,2]{0,6,5,4,3,2,1:T(2,128)} %bitcast.21, f32[]{:T(128)} %constant.28.clone.1), dimensions={2,4,6}, to_apply=%region_0.0 | reduce | flops 114688 | bytes 589828 | tf_op jit(solution)/shard_map/reduce_sum | solution.py:67
  194.1 11.4 %all-to-all-start = ((f32[128,1,256]{2,1,0:T(1,128)}), f32[128,1,256]{2,1,0:T(1,128)S(1)}, u32[]{:S(2)}, u32[]{:S(2)}) async-start(f32[128,1,256]{2,1,0:T(1,128)} %reshape.129), calls=%async_computation | async-start | bytes 262144 | tf_op jit(solution)/shard_map/all_to_all | solution.py:143
  205.6 62.0 %all-gather = f32[256,2,16]{2,1,0:T(2,128)S(1)} all-gather(f32[2,2,16]{2,1,0:T(2,128)S(1)} %multiply_add_fusion.2), channel_id=2, replica_groups=mesh['gx_0'=4,'gx_1'=2,'gy'=4,'gz'=4] {'gx_0','gx_1','gy','gz'}, dimensions={0}, use_global_device_ids=true | all-gather | bytes 33024 | tf_op jit(solution)/shard_map/all_gather | solution.py:134
  317.5 6.2 collective-permute-start.49
  343.0 6.2 collective-permute-start.55
  370.7 8.9 broadcast_in_dim.14
  379.6 10.0 copy.2416
  389.7 6.2 collective-permute-start.61
  473.4 7.5 all-reduce.83
  486.9 10.6 %all-reduce.81 = (f32[4]{0:T(128)S(1)}, f32[4]{0:T(128)S(1)}) all-reduce(f32[4]{0:T(128)S(1)} %get-tuple-element.32, f32[4]{0:T(128)S(1)} %get-tuple-element.33), channel_id=1, replica_groups=mesh['gx_0'=4,'gx_1'=2,'gy'=4,'gz'=4] {'gy'}, use_global_device_ids=true, to_apply=%region_9.10 | all-reduce | flops 8 | bytes 64 | tf_op jit(solution)/shard_map/psum | solution.py:50
  564.3 8.7 copy.2467
  573.1 13.1 %reduce_sum.134 = f32[4,8,8,64]{0,3,2,1:T(8,128)} reduce(f32[4,8,2,8,2,64,2]{0,6,5,4,3,2,1:T(2,128)} %bitcast.23, f32[]{:T(128)} %constant.28.clone.1), dimensions={2,4,6}, to_apply=%region_16.17 | reduce | flops 114688 | bytes 589828 | tf_op jit(solution)/shard_map/reduce_sum | solution.py:67
  665.9 6.2 collective-permute-start.109
  693.1 21.0 %all_to_all.10 = f32[128,1,256]{2,1,0:T(1,128)S(1)} all-to-all(f32[128,1,256]{2,1,0:T(1,128)S(1)} %reshape.131), channel_id=1, replica_groups=mesh['gx_0'=4,'gx_1'=2,'gy'=4,'gz'=4] {'gx_0','gx_1','gy','gz'}, dimensions={0} | all-to-all | bytes 262144 | tf_op jit(solution)/shard_map/all_to_all | solution.py:143
  741.8 6.2 collective-permute-start.121
  769.4 6.2 collective-permute-start.127
  794.9 6.2 collective-permute-start.133
  822.6 8.9 broadcast_in_dim.17
  831.5 10.0 copy.2478
  931.0 6.3 all-reduce.84
  937.4 10.6 %all-reduce.80 = (f32[4]{0:T(128)S(1)}, f32[4]{0:T(128)S(1)}) all-reduce(f32[4]{0:T(128)S(1)} %get-tuple-element.30, f32[4]{0:T(128)S(1)} %get-tuple-element.31), channel_id=1, replica_groups=mesh['gx_0'=4,'gx_1'=2,'gy'=4,'gz'=4] {'gy'}, use_global_device_ids=true, to_apply=%region_22.23 | all-reduce | flops 8 | bytes 64 | tf_op jit(solution)/shard_map/psum | solution.py:50
  956.1 65.5 %psum.135 = f32[4]{0:T(128)S(1)} all-reduce(f32[4]{0:T(128)S(1)} %get-tuple-element.200), channel_id=1, replica_groups=mesh['gx_0'=4,'gx_1'=2,'gy'=4,'gz'=4] {'gx_0','gx_1','gy','gz'}, use_global_device_ids=true, to_apply=%region_30.31 | all-reduce | flops 4 | bytes 32 | tf_op jit(solution)/shard_map/psum | solution.py:207
  (640 shorter events, 688.4 us)
Async XLA Ops:
  41.2 19.9 %collective-permute-start.9 = (f32[4,18,16,1]{1,2,3,0:T(8,128)S(1)}, f32[4,18,16,1]{1,2,3,0:T(8,128)S(1)}, u32[]{:S(2)}, u32[]{:S(2)}) collective-permute-start(f32[4,18,16,1]{1,2,3,0:T(8,128)S(1)} %copy.2394), channel_id=1, source_target_pairs={{4,0},{8,4},{12,8},{5,1},{9,5},{13,9},{6,2},{10,6},{14,10},{7,3},{... | collective-permute-start | bytes 13832 | tf_op jit(solution)/shard_map/ppermute | solution.py:23
  96.1 23.9 %collective-permute-start.13 = (f32[4,1,8,64]{3,2,1,0:T(8,128)S(1)}, f32[4,1,8,64]{3,2,1,0:T(8,128)S(1)}, u32[]{:S(2)}, u32[]{:S(2)}) collective-permute-start(f32[4,1,8,64]{3,2,1,0:T(8,128)S(1)} %get-tuple-element.194), channel_id=1, source_target_pairs={{0,16},{16,32},{32,48},{48,64},{64,80},{80,96},{96,112},{1,17},{17... | collective-permute-start | bytes 24584 | tf_op jit(solution)/shard_map/ppermute | solution.py:36
  100.3 19.6 %collective-permute-start.12 = (f32[4,1,8,64]{3,2,1,0:T(8,128)S(1)}, f32[4,1,8,64]{3,2,1,0:T(8,128)S(1)}, u32[]{:S(2)}, u32[]{:S(2)}) collective-permute-start(f32[4,1,8,64]{3,2,1,0:T(8,128)S(1)} %get-tuple-element.195), channel_id=1, source_target_pairs={{16,0},{32,16},{48,32},{64,48},{80,64},{96,80},{112,96},{17,1},{33... | collective-permute-start | bytes 24584 | tf_op jit(solution)/shard_map/ppermute | solution.py:37
  121.7 19.2 %collective-permute-start.19 = (f32[4,1,8,64]{3,2,1,0:T(8,128)S(1)}, f32[4,1,8,64]{3,2,1,0:T(8,128)S(1)}, u32[]{:S(2)}, u32[]{:S(2)}) collective-permute-start(f32[4,1,8,64]{3,2,1,0:T(8,128)S(1)} %get-tuple-element.188), channel_id=1, source_target_pairs={{0,16},{16,32},{32,48},{48,64},{64,80},{80,96},{96,112},{1,17},{17... | collective-permute-start | bytes 24584 | tf_op jit(solution)/shard_map/ppermute | solution.py:36
  146.5 21.8 %collective-permute-start.25 = (f32[4,1,4,32]{0,3,2,1:T(8,128)S(1)}, f32[4,1,4,32]{0,3,2,1:T(8,128)S(1)}, u32[]{:S(2)}, u32[]{:S(2)}) collective-permute-start(f32[4,1,4,32]{0,3,2,1:T(8,128)S(1)} %get-tuple-element.146), channel_id=1, source_target_pairs={{0,16},{16,32},{32,48},{48,64},{64,80},{80,96},{96,112},{1,17},{17... | collective-permute-start | bytes 6152 | tf_op jit(solution)/shard_map/ppermute | solution.py:36
  168.6 22.6 %collective-permute-start.31 = (f32[4,1,4,32]{0,3,2,1:T(8,128)S(1)}, f32[4,1,4,32]{0,3,2,1:T(8,128)S(1)}, u32[]{:S(2)}, u32[]{:S(2)}) collective-permute-start(f32[4,1,4,32]{0,3,2,1:T(8,128)S(1)} %get-tuple-element.140), channel_id=1, source_target_pairs={{0,16},{16,32},{32,48},{48,64},{64,80},{80,96},{96,112},{1,17},{17... | collective-permute-start | bytes 6152 | tf_op jit(solution)/shard_map/ppermute | solution.py:36
  194.1 73.8 %all-to-all-start = ((f32[128,1,256]{2,1,0:T(1,128)}), f32[128,1,256]{2,1,0:T(1,128)S(1)}, u32[]{:S(2)}, u32[]{:S(2)}) async-start(f32[128,1,256]{2,1,0:T(1,128)} %reshape.129), calls=%async_computation | async-start | bytes 262144 | tf_op jit(solution)/shard_map/all_to_all | solution.py:143
  290.7 21.8 %collective-permute-start.43 = (f32[4,1,4,32]{0,3,2,1:T(8,128)S(1)}, f32[4,1,4,32]{0,3,2,1:T(8,128)S(1)}, u32[]{:S(2)}, u32[]{:S(2)}) collective-permute-start(f32[4,1,4,32]{0,3,2,1:T(8,128)S(1)} %get-tuple-element.128), channel_id=1, source_target_pairs={{0,16},{16,32},{32,48},{48,64},{64,80},{80,96},{96,112},{1,17},{17... | collective-permute-start | bytes 6152 | tf_op jit(solution)/shard_map/ppermute | solution.py:36
  317.5 25.1 %collective-permute-start.49 = (f32[4,1,8,64]{3,2,1,0:T(8,128)S(1)}, f32[4,1,8,64]{3,2,1,0:T(8,128)S(1)}, u32[]{:S(2)}, u32[]{:S(2)}) collective-permute-start(f32[4,1,8,64]{3,2,1,0:T(8,128)S(1)} %get-tuple-element.182), channel_id=1, source_target_pairs={{0,16},{16,32},{32,48},{48,64},{64,80},{80,96},{96,112},{1,17},{17... | collective-permute-start | bytes 24584 | tf_op jit(solution)/shard_map/ppermute | solution.py:36
  323.7 18.9 %collective-permute-start.48 = (f32[4,1,8,64]{3,2,1,0:T(8,128)S(1)}, f32[4,1,8,64]{3,2,1,0:T(8,128)S(1)}, u32[]{:S(2)}, u32[]{:S(2)}) collective-permute-start(f32[4,1,8,64]{3,2,1,0:T(8,128)S(1)} %get-tuple-element.183), channel_id=1, source_target_pairs={{16,0},{32,16},{48,32},{64,48},{80,64},{96,80},{112,96},{17,1},{33... | collective-permute-start | bytes 24584 | tf_op jit(solution)/shard_map/ppermute | solution.py:37
  343.0 25.3 %collective-permute-start.55 = (f32[4,1,8,64]{3,2,1,0:T(8,128)S(1)}, f32[4,1,8,64]{3,2,1,0:T(8,128)S(1)}, u32[]{:S(2)}, u32[]{:S(2)}) collective-permute-start(f32[4,1,8,64]{3,2,1,0:T(8,128)S(1)} %get-tuple-element.176), channel_id=1, source_target_pairs={{0,16},{16,32},{32,48},{48,64},{64,80},{80,96},{96,112},{1,17},{17... | collective-permute-start | bytes 24584 | tf_op jit(solution)/shard_map/ppermute | solution.py:36
  349.2 19.1 %collective-permute-start.54 = (f32[4,1,8,64]{3,2,1,0:T(8,128)S(1)}, f32[4,1,8,64]{3,2,1,0:T(8,128)S(1)}, u32[]{:S(2)}, u32[]{:S(2)}) collective-permute-start(f32[4,1,8,64]{3,2,1,0:T(8,128)S(1)} %get-tuple-element.177), channel_id=1, source_target_pairs={{16,0},{32,16},{48,32},{64,48},{80,64},{96,80},{112,96},{17,1},{33... | collective-permute-start | bytes 24584 | tf_op jit(solution)/shard_map/ppermute | solution.py:37
  588.5 24.7 %collective-permute-start.91 = (f32[4,1,8,64]{3,2,1,0:T(8,128)S(1)}, f32[4,1,8,64]{3,2,1,0:T(8,128)S(1)}, u32[]{:S(2)}, u32[]{:S(2)}) collective-permute-start(f32[4,1,8,64]{3,2,1,0:T(8,128)S(1)} %get-tuple-element.170), channel_id=1, source_target_pairs={{0,16},{16,32},{32,48},{48,64},{64,80},{80,96},{96,112},{1,17},{17... | collective-permute-start | bytes 24584 | tf_op jit(solution)/shard_map/ppermute | solution.py:36
  592.6 20.7 %collective-permute-start.90 = (f32[4,1,8,64]{3,2,1,0:T(8,128)S(1)}, f32[4,1,8,64]{3,2,1,0:T(8,128)S(1)}, u32[]{:S(2)}, u32[]{:S(2)}) collective-permute-start(f32[4,1,8,64]{3,2,1,0:T(8,128)S(1)} %get-tuple-element.171), channel_id=1, source_target_pairs={{16,0},{32,16},{48,32},{64,48},{80,64},{96,80},{112,96},{17,1},{33... | collective-permute-start | bytes 24584 | tf_op jit(solution)/shard_map/ppermute | solution.py:37
  594.5 18.7 %collective-permute-start.94 = (f32[4,8,1,64]{3,2,1,0:T(1,128)S(1)}, f32[4,8,1,64]{3,2,1,0:T(1,128)S(1)}, u32[]{:S(2)}, u32[]{:S(2)}) collective-permute-start(f32[4,8,1,64]{3,2,1,0:T(1,128)S(1)} %get-tuple-element.166), channel_id=1, source_target_pairs={{1,0},{2,1},{3,2},{5,4},{6,5},{7,6},{9,8},{10,9},{11,10},{13,12},{... | collective-permute-start | bytes 24584 | tf_op jit(solution)/shard_map/ppermute | solution.py:37
  613.6 24.3 %collective-permute-start.97 = (f32[4,1,8,64]{3,2,1,0:T(8,128)S(1)}, f32[4,1,8,64]{3,2,1,0:T(8,128)S(1)}, u32[]{:S(2)}, u32[]{:S(2)}) collective-permute-start(f32[4,1,8,64]{3,2,1,0:T(8,128)S(1)} %get-tuple-element.164), channel_id=1, source_target_pairs={{0,16},{16,32},{32,48},{48,64},{64,80},{80,96},{96,112},{1,17},{17... | collective-permute-start | bytes 24584 | tf_op jit(solution)/shard_map/ppermute | solution.py:36
  618.3 19.6 %collective-permute-start.96 = (f32[4,1,8,64]{3,2,1,0:T(8,128)S(1)}, f32[4,1,8,64]{3,2,1,0:T(8,128)S(1)}, u32[]{:S(2)}, u32[]{:S(2)}) collective-permute-start(f32[4,1,8,64]{3,2,1,0:T(8,128)S(1)} %get-tuple-element.165), channel_id=1, source_target_pairs={{16,0},{32,16},{48,32},{64,48},{80,64},{96,80},{112,96},{17,1},{33... | collective-permute-start | bytes 24584 | tf_op jit(solution)/shard_map/ppermute | solution.py:37
  643.5 22.1 %collective-permute-start.103 = (f32[4,1,4,32]{0,3,2,1:T(8,128)S(1)}, f32[4,1,4,32]{0,3,2,1:T(8,128)S(1)}, u32[]{:S(2)}, u32[]{:S(2)}) collective-permute-start(f32[4,1,4,32]{0,3,2,1:T(8,128)S(1)} %get-tuple-element.122), channel_id=1, source_target_pairs={{0,16},{16,32},{32,48},{48,64},{64,80},{80,96},{96,112},{1,17},{17... | collective-permute-start | bytes 6152 | tf_op jit(solution)/shard_map/ppermute | solution.py:36
  665.9 22.7 %collective-permute-start.109 = (f32[4,1,4,32]{0,3,2,1:T(8,128)S(1)}, f32[4,1,4,32]{0,3,2,1:T(8,128)S(1)}, u32[]{:S(2)}, u32[]{:S(2)}) collective-permute-start(f32[4,1,4,32]{0,3,2,1:T(8,128)S(1)} %get-tuple-element.116), channel_id=1, source_target_pairs={{0,16},{16,32},{32,48},{48,64},{64,80},{80,96},{96,112},{1,17},{17... | collective-permute-start | bytes 6152 | tf_op jit(solution)/shard_map/ppermute | solution.py:36
  741.8 22.6 %collective-permute-start.121 = (f32[4,1,4,32]{0,3,2,1:T(8,128)S(1)}, f32[4,1,4,32]{0,3,2,1:T(8,128)S(1)}, u32[]{:S(2)}, u32[]{:S(2)}) collective-permute-start(f32[4,1,4,32]{0,3,2,1:T(8,128)S(1)} %get-tuple-element.104), channel_id=1, source_target_pairs={{0,16},{16,32},{32,48},{48,64},{64,80},{80,96},{96,112},{1,17},{17... | collective-permute-start | bytes 6152 | tf_op jit(solution)/shard_map/ppermute | solution.py:36
  769.4 25.1 %collective-permute-start.127 = (f32[4,1,8,64]{3,2,1,0:T(8,128)S(1)}, f32[4,1,8,64]{3,2,1,0:T(8,128)S(1)}, u32[]{:S(2)}, u32[]{:S(2)}) collective-permute-start(f32[4,1,8,64]{3,2,1,0:T(8,128)S(1)} %get-tuple-element.158), channel_id=1, source_target_pairs={{0,16},{16,32},{32,48},{48,64},{64,80},{80,96},{96,112},{1,17},{17... | collective-permute-start | bytes 24584 | tf_op jit(solution)/shard_map/ppermute | solution.py:36
  775.6 18.9 %collective-permute-start.126 = (f32[4,1,8,64]{3,2,1,0:T(8,128)S(1)}, f32[4,1,8,64]{3,2,1,0:T(8,128)S(1)}, u32[]{:S(2)}, u32[]{:S(2)}) collective-permute-start(f32[4,1,8,64]{3,2,1,0:T(8,128)S(1)} %get-tuple-element.159), channel_id=1, source_target_pairs={{16,0},{32,16},{48,32},{64,48},{80,64},{96,80},{112,96},{17,1},{33... | collective-permute-start | bytes 24584 | tf_op jit(solution)/shard_map/ppermute | solution.py:37
  794.9 25.3 %collective-permute-start.133 = (f32[4,1,8,64]{3,2,1,0:T(8,128)S(1)}, f32[4,1,8,64]{3,2,1,0:T(8,128)S(1)}, u32[]{:S(2)}, u32[]{:S(2)}) collective-permute-start(f32[4,1,8,64]{3,2,1,0:T(8,128)S(1)} %get-tuple-element.152), channel_id=1, source_target_pairs={{0,16},{16,32},{32,48},{48,64},{64,80},{80,96},{96,112},{1,17},{17... | collective-permute-start | bytes 24584 | tf_op jit(solution)/shard_map/ppermute | solution.py:36
  801.1 19.1 %collective-permute-start.132 = (f32[4,1,8,64]{3,2,1,0:T(8,128)S(1)}, f32[4,1,8,64]{3,2,1,0:T(8,128)S(1)}, u32[]{:S(2)}, u32[]{:S(2)}) collective-permute-start(f32[4,1,8,64]{3,2,1,0:T(8,128)S(1)} %get-tuple-element.153), channel_id=1, source_target_pairs={{16,0},{32,16},{48,32},{64,48},{80,64},{96,80},{112,96},{17,1},{33... | collective-permute-start | bytes 24584 | tf_op jit(solution)/shard_map/ppermute | solution.py:37
  (143 other events, 1363.6 us)
